TPU v7x, 32 devices: a whole 2x2x4 slice. The times are simulated.
32 devices in a mesh: expert: 4 (over y, x), shard: 8 (over z, core).
Axes of the slice: x: 2, y: 2, z: 4, core: 2. Of those that a mesh axis runs over, the one named last changes fastest.
Arguments:
- master_gate: float32 [128, 2048, 768], P('expert', 'shard'), may hold values from -0.1875 to 0.1875
- second_gate: bfloat16 [128, 2048, 768], P('expert', 'shard'), may hold values from -0.0625 to 0.0625
- master_up: float32 [128, 2048, 768], P('expert', 'shard'), may hold values from -0.1875 to 0.1875
- second_up: bfloat16 [128, 2048, 768], P('expert', 'shard'), may hold values from -0.0625 to 0.0625
- router_weight: float32 [2048, 128], P('shard', 'expert'), may hold values from -0.125 to 0.125
- router_gain: float32 [2048], P('shard'), may hold values from 0.25 to 1.75
Outputs:
- final_gate: bfloat16 [128, 2048, 768], P(('expert', 'shard'))
- final_up: bfloat16 [128, 2048, 768], P(('expert', 'shard'))
- scale_gate: float32 [128, 768], P(('expert', 'shard'))
- scale_up: float32 [128, 768], P(('expert', 'shard'))
- serve_router: bfloat16 [2048, 128], replicated
All inputs are finite; a program needn't handle non-finite values. Where the computation divides by a largest or mean magnitude, that divisor is 1e-20 or more.
Results may differ from a plain program's by a relative error of at most 0.0085.
Values may be sent and summed in bfloat16 or wider, within the bound.
A program may use at most 192 MiB of HBM per device.

v0:
```python
import jax
import jax.numpy as jnp
from jax import lax
from jax.sharding import PartitionSpec as P

D_MODEL = 2048


def shards(master_gate, second_gate, master_up, second_up, router_weight, router_gain):
    merged_gate = master_gate + second_gate.astype(jnp.float32)
    merged_up = master_up + second_up.astype(jnp.float32)
    whole_gate, whole_up = (
        lax.all_to_all(
            merged_gate.astype(jnp.bfloat16), "shard", split_axis=0, concat_axis=1, tiled=True
        ).astype(merged_gate.dtype),
        lax.all_to_all(
            merged_up.astype(jnp.bfloat16), "shard", split_axis=0, concat_axis=1, tiled=True
        ).astype(merged_up.dtype),
    )
    scale_gate = jnp.sum(jnp.abs(whole_gate), axis=1) / D_MODEL
    final_gate = (whole_gate / jnp.expand_dims(scale_gate, 1)).astype(jnp.bfloat16)
    scale_up = jnp.sum(jnp.abs(whole_up), axis=1) / D_MODEL
    final_up = (whole_up / jnp.expand_dims(scale_up, 1)).astype(jnp.bfloat16)
    part_router = (router_weight * router_gain[:, None]).astype(jnp.bfloat16)
    row_router = lax.all_gather(part_router, "shard", axis=0, tiled=True)
    serve_router = lax.all_gather(row_router, "expert", axis=1, tiled=True)
    return (final_gate, final_up, scale_gate, scale_up, serve_router)


def solution(mesh):
    in_specs = (
        P("expert", "shard", None),
        P("expert", "shard", None),
        P("expert", "shard", None),
        P("expert", "shard", None),
        P("shard", "expert"),
        P("shard"),
    )
    out_specs = (
        P(("expert", "shard"), None, None),
        P(("expert", "shard"), None, None),
        P(("expert", "shard"), None),
        P(("expert", "shard"), None),
        P(),
    )
    return jax.shard_map(shards, mesh=mesh, in_specs=in_specs, out_specs=out_specs, check_vma=False)
```

profile of v0, /device:TPU:0, one launch (start us, length us, event | category | flops | bytes accessed | tf_op | source)
XLA Modules:
  0.0 651.9 jit_solution(11596359484674669892)
XLA Ops:
  0.6 17.4 %add_convert_fusion = bf16[32,256,768]{2,1,0:T(8,128)(2,1)} fusion(f32[32,256,768]{2,1,0:T(8,128)} %param.8, bf16[32,256,768]{2,1,0:T(8,128)(2,1)} %param.9), kind=kLoop, calls=%fused_computation.5 | loop fusion | flops 18874368 | bytes 50331648 | tf_op jit(solution)/shard_map/convert_element_type | solution.py:17
  18.0 6.4 all-to-all-start.1
  24.4 17.4 %add_convert_fusion.1 = bf16[32,256,768]{2,1,0:T(8,128)(2,1)} fusion(f32[32,256,768]{2,1,0:T(8,128)} %param.6, bf16[32,256,768]{2,1,0:T(8,128)(2,1)} %param.7), kind=kLoop, calls=%fused_computation.7 | loop fusion | flops 18874368 | bytes 50331648 | tf_op jit(solution)/shard_map/convert_element_type | solution.py:14
  41.7 0.0 copy-start.2
  41.7 0.0 copy-start.3
  41.7 256.5 %all-to-all-done.1 = bf16[32,256,768]{2,1,0:T(8,128)(2,1)} async-done(((bf16[32,256,768]{2,1,0:T(8,128)(2,1)}), bf16[32,256,768]{2,1,0:T(8,128)(2,1)}, u32[]{:S(2)}, u32[]{:S(2)}) %all-to-all-start.1) | async-done | bytes 12582944 | tf_op jit(solution)/shard_map/all_to_all | solution.py:16
  298.2 5.4 all-to-all-start
  303.7 0.0 copy-done.2
  303.7 0.0 copy-done.3
  303.7 280.0 %all_gather.6 = bf16[2048,32]{0,1:T(8,128)(2,1)S(1)} all-gather(bf16[256,32]{0,1:T(8,128)(2,1)S(1)} %multiply_convert_fusion), channel_id=1, replica_groups=mesh['expert'=4,'shard'=8] {'shard'}, dimensions={0}, use_global_device_ids=true | all-gather | bytes 147456 | tf_op jit(solution)/shard_map/all_gather | solution.py:25
  583.7 10.7 %all_gather.7 = bf16[2048,128]{0,1:T(8,128)(2,1)S(1)} all-gather(bf16[2048,32]{0,1:T(8,128)(2,1)S(1)} %all_gather.6), channel_id=1, replica_groups=mesh['expert'=4,'shard'=8] {'expert'}, dimensions={1}, use_global_device_ids=true | all-gather | bytes 655360 | tf_op jit(solution)/shard_map/all_gather | solution.py:26
  594.3 1.0 copy.24
  595.3 7.2 %abs_reduce_fusion = f32[32,768]{1,0:T(8,128)S(1)} fusion(bf16[32,256,768]{2,1,0:T(8,128)(2,1)} %all-to-all-done.1), kind=kLoop, calls=%fused_computation.4 | loop fusion | flops 18849792 | bytes 12681216 | tf_op jit(solution)/shard_map/reduce_sum | solution.py:22
  602.5 14.7 %copy.22 = f32[8,4,256,768]{3,2,0,1:T(8,128)} copy(bf16[8,4,256,768]{3,2,1,0:T(8,128)(2,1)} %bitcast.15) | data formatting | bytes 37748736 | tf_op jit(solution)/shard_map/convert_element_type | solution.py:18
  617.2 0.0 copy-start
  617.2 0.0 all-to-all-done
  617.2 7.2 %abs_reduce_fusion.1 = f32[32,768]{1,0:T(8,128)S(1)} fusion(bf16[32,256,768]{2,1,0:T(8,128)(2,1)} %all-to-all-done), kind=kLoop, calls=%fused_computation.6 | loop fusion | flops 18849792 | bytes 12681216 | tf_op jit(solution)/shard_map/reduce_sum | solution.py:20
  624.5 0.0 copy-start.1
  624.5 7.3 %copy.20 = f32[8,4,256,768]{3,2,0,1:T(8,128)S(1)} copy(bf16[8,4,256,768]{3,2,1,0:T(8,128)(2,1)} %bitcast.14) | data formatting | bytes 37748736 | tf_op jit(solution)/shard_map/convert_element_type | solution.py:15
  631.8 0.0 copy-done
  631.8 13.4 %fusion = bf16[4,2048,768]{2,1,0:T(8,128)(2,1)} fusion(f32[8,4,256,768]{3,2,0,1:T(8,128)} %copy.22, f32[4,768]{1,0:T(4,128)S(1)} %broadcast_multiply_fusion), kind=kLoop, calls=%fused_computation.1 | loop fusion | flops 12582912 | bytes 37761024 | tf_op jit(solution)/shard_map/convert_element_type | solution.py:23
  645.2 0.0 copy-done.1
  645.2 6.7 %fusion.1 = bf16[4,2048,768]{2,1,0:T(8,128)(2,1)} fusion(f32[8,4,256,768]{3,2,0,1:T(8,128)S(1)} %copy.20, f32[4,768]{1,0:T(4,128)S(1)} %broadcast_multiply_fusion.1), kind=kLoop, calls=%fused_computation.3 | loop fusion | flops 12582912 | bytes 37761024 | tf_op jit(solution)/shard_map/convert_element_type | solution.py:21
  (7 shorter events, 0.1 us)
Async XLA Ops:
  18.0 280.2 %all-to-all-start.1 = ((bf16[32,256,768]{2,1,0:T(8,128)(2,1)}), bf16[32,256,768]{2,1,0:T(8,128)(2,1)}, u32[]{:S(2)}, u32[]{:S(2)}) async-start(bf16[32,256,768]{2,1,0:T(8,128)(2,1)} %add_convert_fusion), calls=%async_computation.1 | async-start | bytes 25165824 | tf_op jit(solution)/shard_map/all_to_all | solution.py:16
  41.7 261.9 %copy-start.2 = (f32[256,32]{0,1:T(8,128)S(1)}, f32[256,32]{0,1:T(8,128)}, u32[]{:S(2)}) copy-start(f32[256,32]{0,1:T(8,128)} %param.10) | copy-start | bytes 98308
  41.7 261.9 %copy-start.3 = (f32[256]{0:T(256)S(1)}, f32[256]{0:T(256)}, u32[]{:S(2)}) copy-start(f32[256]{0:T(256)} %param.11) | copy-start | bytes 3076
  298.2 319.0 %all-to-all-start = ((bf16[32,256,768]{2,1,0:T(8,128)(2,1)}), bf16[32,256,768]{2,1,0:T(8,128)(2,1)}, u32[]{:S(2)}, u32[]{:S(2)}) async-start(bf16[32,256,768]{2,1,0:T(8,128)(2,1)} %add_convert_fusion.1), calls=%async_computation | async-start | bytes 25165824 | tf_op jit(solution)/shard_map/all_to_all | solution.py:13
  617.2 14.6 %copy-start = (f32[4,768]{1,0:T(4,128)}, f32[4,768]{1,0:T(4,128)S(1)}, u32[]{:S(2)}) copy-start(f32[4,768]{1,0:T(4,128)S(1)} %broadcast_multiply_fusion) | copy-start | bytes 36868
  624.5 20.7 %copy-start.1 = (f32[4,768]{1,0:T(4,128)}, f32[4,768]{1,0:T(4,128)S(1)}, u32[]{:S(2)}) copy-start(f32[4,768]{1,0:T(4,128)S(1)} %broadcast_multiply_fusion.1) | copy-start | bytes 36868
where the time goes:
time: 652 us
  blocking collectives  291 us (45%)
  waiting for transfers between devices  256 us (39%)
  other arithmetic  69.2 us (11%)
  local copies, waits for them, and re-layouts  23 us (4%)
  starting transfers between devices  11.8 us (2%)
    all_gather x1, blocking collectives, shards(): row_router = lax.all_gather(part_router, 'shard', axis=0, tiled=True)  280 us
    all_to_all x1, waiting for transfers between devices, shards(): lax.all_to_all(merged_up.astype(jnp.bfloat16), 'shard', split_axis=0, con...  256 us
    convert_element_type x2, local copies, waits for them, and re-layouts, shards(): whole_gate, whole_up = (lax.all_to_all(merged_gate.astype(jnp.bfloat16),...  21.9 us
    convert_element_type x1, other arithmetic, shards(): merged_up.astype(jnp.bfloat16)  17.4 us
    convert_element_type x1, other arithmetic, shards(): merged_gate.astype(jnp.bfloat16)  17.4 us
    convert_element_type x1, other arithmetic, shards(): final_up = (whole_up / jnp.expand_dims(scale_up, 1)).astype(jnp.bfloat16)  13.4 us
  transfers between devices with their start and end apart: 2, of which 1 were waited for; matrix products, arithmetic and copies ran while one was open for 6% of the time, Pallas kernels for 0%

commit v1 on v0

v1 whole, which is shorter than its diff:
```python
import functools

import jax
import jax.numpy as jnp
from jax import lax
from jax.experimental import pallas as pl
from jax.experimental.pallas import tpu as pltpu
from jax.sharding import PartitionSpec as P

MESH = pl.DeviceIdType.MESH
SLOTS = 3
STRIP = 64


def exchange(
    groups, n, each, rows, width,
    master_gate, second_gate, master_up, second_up, router,
    final_gate, final_up, scale_gate, scale_up, routed,
    land_gate, land_up, out_sem, sent, wide, narrow, in_sem, send_sem, recv_sem, row_send, row_recv, col_send, col_recv,
):
    group, me = lax.axis_index("expert"), lax.axis_index("shard")
    half = n // 2
    near = half - 2
    n_remote = each * (n - 1)
    n_items = each * n
    base = (me // half) * half
    chip = me // 2
    outer = ((chip == 0) | (chip == half - 1)).astype(jnp.int32)

    def item(i):
        cross_start = outer * (each * near)
        near_start = (1 - outer) * (each * half)
        is_cross = (i >= cross_start) & (i < cross_start + each * half)
        is_near = (i >= near_start) & (i < near_start + each * near)
        is_pair = (i >= each * (n - 2)) & (i < n_remote)
        q = i - cross_start
        cross_to = lax.rem(base + half + lax.rem(q + me + n_items, half), n)
        cross_j = q // half
        p = i - near_start
        near_to = base + lax.rem((me - base) // 2 * 2 + 2 + lax.rem(p + n_items * near, near), half)
        near_j = p // near
        pair_to = me + 1 - 2 * lax.rem(me, 2)
        pair_j = i - each * (n - 2)
        own_j = i - n_remote
        target = jnp.where(is_cross, cross_to, jnp.where(is_near, near_to, jnp.where(is_pair, pair_to, me)))
        j = jnp.where(is_cross, cross_j, jnp.where(is_near, near_j, jnp.where(is_pair, pair_j, own_j)))
        return target, j

    sources = ((master_gate, second_gate), (master_up, second_up))
    lands = (land_gate, land_up)

    def reads(i):
        target, j = item(i)
        slot = lax.rem(i, SLOTS)
        e = target * each + j
        return [
            pltpu.make_async_copy(ref.at[e], held.at[slot, t], in_sem.at[slot, t, k])
            for t in range(2)
            for k, (ref, held) in enumerate(zip(sources[t], (wide, narrow)))
        ]

    def my_rows():
        return pl.ds(pl.multiple_of(me * rows, rows), rows)

    def sends(i):
        target, j = item(i)
        return [
            pltpu.make_async_remote_copy(
                src_ref=sent.at[i, t],
                dst_ref=lands[t].at[j, my_rows()],
                send_sem=send_sem.at[i, t],
                recv_sem=recv_sem.at[j, t, me],
                device_id=(group, target),
                device_id_type=MESH,
            )
            for t in range(2)
        ]

    for i in range(SLOTS):
        for copy in reads(jnp.int32(i)):
            copy.start()

    barrier = pltpu.get_barrier_semaphore()
    for k in range(1, n):
        pl.semaphore_signal(barrier, inc=1, device_id=(group, lax.rem(me + k, n)), device_id_type=MESH)
    for k in range(1, groups):
        pl.semaphore_signal(barrier, inc=1, device_id=(lax.rem(group + k, groups), me), device_id_type=MESH)
    pl.semaphore_wait(barrier, n + groups - 2)

    def row_copy(k):
        return pltpu.make_async_remote_copy(
            src_ref=router,
            dst_ref=routed.at[group, :, my_rows()],
            send_sem=row_send.at[k],
            recv_sem=row_recv.at[k],
            device_id=(group, lax.rem(me + k + 1, n)),
            device_id_type=MESH,
        )

    def col_copy(k):
        return pltpu.make_async_remote_copy(
            src_ref=routed.at[group],
            dst_ref=routed.at[group],
            send_sem=col_send.at[k],
            recv_sem=col_recv.at[k],
            device_id=(lax.rem(group + k + 1, groups), me),
            device_id_type=MESH,
        )

    def merge(i, put):
        slot = lax.rem(i, SLOTS)
        for t in range(2):
            def strip(s, carry, t=t):
                at = pl.ds(pl.multiple_of(s * STRIP, STRIP), STRIP)
                total = wide[slot, t, at, :] + narrow[slot, t, at, :].astype(jnp.float32)
                put(t, s, total.astype(jnp.bfloat16))
                return carry
            lax.fori_loop(0, rows // STRIP, strip, 0)

    def produce(i, carry):
        for copy in reads(i):
            copy.wait()

        @pl.when(i < n_remote)
        def _():
            def put(t, s, value):
                sent[i, t, pl.ds(pl.multiple_of(s * STRIP, STRIP), STRIP), :] = value
            merge(i, put)

        @pl.when(i >= n_remote)
        def _():
            def put(t, s, value):
                lands[t][i - n_remote, pl.ds(pl.multiple_of(me * rows + s * STRIP, STRIP), STRIP), :] = value
            merge(i, put)

        @pl.when(i + SLOTS < n_items)
        def _():
            for copy in reads(i + SLOTS):
                copy.start()

        @pl.when((i >= 1) & (i <= n_remote))
        def _():
            for copy in sends(i - 1):
                copy.start()
        return carry

    lax.fori_loop(0, n_items, produce, 0)

    for k in range(n - 1):
        row_copy(k).start()
    routed[group, :, my_rows()] = router[...]
    for k in range(n - 1):
        row_copy(k).wait()
    for k in range(groups - 1):
        col_copy(k).start()

    scales = (scale_gate, scale_up)
    d_model = n * rows

    def put_out(j, t):
        return pltpu.make_async_copy(lands[t].at[j], (final_gate, final_up)[t].at[j], out_sem.at[j, t])

    def finish(j, carry):
        for t in range(2):
            land = lands[t]

            def arrive(k, c, t=t):
                source = lax.rem(me + 1 + k, n)
                pltpu.make_async_remote_copy(
                    src_ref=sent.at[0, t],
                    dst_ref=lands[t].at[j, pl.ds(pl.multiple_of(source * rows, rows), rows)],
                    send_sem=send_sem.at[0, t],
                    recv_sem=recv_sem.at[j, t, source],
                    device_id=(group, source),
                    device_id_type=MESH,
                ).wait_recv()
                return c

            lax.fori_loop(0, n - 1, arrive, 0)

            def add(s, total, land=land):
                at = pl.ds(pl.multiple_of(s * STRIP, STRIP), STRIP)
                block = jnp.abs(land[j, at, :].astype(jnp.float32))
                return total + jnp.sum(block.reshape(STRIP // 8, 8, width), axis=0)

            total = lax.fori_loop(0, d_model // STRIP, add, jnp.zeros((8, width), jnp.float32))
            scale = jnp.sum(total, axis=0, keepdims=True) / d_model
            scales[t][j] = scale
            factor = jnp.broadcast_to(1.0 / scale, (STRIP, width))

            def divide(s, c, land=land, factor=factor):
                at = pl.ds(pl.multiple_of(s * STRIP, STRIP), STRIP)
                land[j, at, :] = (land[j, at, :].astype(jnp.float32) * factor).astype(jnp.bfloat16)
                return c

            lax.fori_loop(0, d_model // STRIP, divide, 0)
            put_out(j, t).start()
        return carry

    lax.fori_loop(0, each, finish, 0)

    for k in range(groups - 1):
        col_copy(k).wait()

    def drain(i, carry):
        for copy in sends(i):
            copy.wait_send()
        return carry

    lax.fori_loop(0, n_remote, drain, 0)
    for j in range(each):
        for t in range(2):
            put_out(j, t).wait()


def shards(groups, n, master_gate, second_gate, master_up, second_up, router_weight, router_gain):
    experts, rows, width = master_gate.shape
    each = experts // n
    columns = router_weight.shape[1]
    router = (router_weight * router_gain[:, None]).astype(jnp.bfloat16).T
    land = pltpu.VMEM((each, n * rows, width), jnp.bfloat16)
    final = jax.ShapeDtypeStruct((each, n * rows, width), jnp.bfloat16)
    scale = jax.ShapeDtypeStruct((each, 1, width), jnp.float32)
    vmem = pl.BlockSpec(memory_space=pltpu.VMEM)
    hbm = pl.BlockSpec(memory_space=pltpu.HBM)
    remote = each * (n - 1)
    final_gate, final_up, scale_gate, scale_up, routed = pl.pallas_call(
        functools.partial(exchange, groups, n, each, rows, width),
        out_shape=(final, final, scale, scale, jax.ShapeDtypeStruct((groups, columns, n * rows), jnp.bfloat16)),
        in_specs=[hbm] * 4 + [vmem],
        out_specs=(hbm, hbm, vmem, vmem, vmem),
        scratch_shapes=[
            land,
            land,
            pltpu.SemaphoreType.DMA((each, 2)),
            pltpu.VMEM((remote, 2, rows, width), jnp.bfloat16),
            pltpu.VMEM((SLOTS, 2, rows, width), jnp.float32),
            pltpu.VMEM((SLOTS, 2, rows, width), jnp.bfloat16),
            pltpu.SemaphoreType.DMA((SLOTS, 2, 2)),
            pltpu.SemaphoreType.DMA((remote, 2)),
            pltpu.SemaphoreType.DMA((each, 2, n)),
            pltpu.SemaphoreType.DMA((n - 1,)),
            pltpu.SemaphoreType.DMA((n - 1,)),
            pltpu.SemaphoreType.DMA((groups - 1,)),
            pltpu.SemaphoreType.DMA((groups - 1,)),
        ],
        compiler_params=pltpu.CompilerParams(
            collective_id=0, has_side_effects=True, vmem_limit_bytes=60 * 1024 * 1024
        ),
    )(master_gate, second_gate, master_up, second_up, router)
    serve_router = routed.reshape(groups * columns, n * rows).T
    return (
        final_gate, final_up,
        scale_gate.reshape(each, width), scale_up.reshape(each, width), serve_router,
    )


def solution(mesh):
    groups, n = mesh.shape["expert"], mesh.shape["shard"]
    in_specs = (
        P("expert", "shard", None),
        P("expert", "shard", None),
        P("expert", "shard", None),
        P("expert", "shard", None),
        P("shard", "expert"),
        P("shard"),
    )
    out_specs = (
        P(("expert", "shard"), None, None),
        P(("expert", "shard"), None, None),
        P(("expert", "shard"), None),
        P(("expert", "shard"), None),
        P(),
    )
    return jax.shard_map(
        functools.partial(shards, groups, n), mesh=mesh, in_specs=in_specs, out_specs=out_specs, check_vma=False
    )
```

time: 652 us -> 591 us (0.906)
  Pallas kernels: 0 us -> 567 us
  blocking collectives: 291 us -> 0 us
  waiting for transfers between devices: 256 us -> 0 us
  other arithmetic: 69.2 us -> 1.37 us
  starting transfers between devices: 11.8 us -> 0 us
    pallas_call x0 -> x1, Pallas kernels: none -> 567 us  [shards(): pl.pallas_call(functools.partial(exchange, groups, n, each, rows, width),...]
    all_gather x2 -> x0, blocking collectives: 291 us -> none  [the longest x1 280 us: shards(): row_router = lax.all_gather(part_router, 'shard', axis=0, tiled=True)]
    all_to_all x2 -> x0, waiting for transfers between devices: 256 us -> none  [the longest x1 256 us: shards(): lax.all_to_all(merged_up.astype(jnp.bfloat16), 'shard', split_axis=0, con...]
    convert_element_type x5 -> x0, other arithmetic: 54.8 us -> none  [the longest x1 17.4 us: shards(): merged_up.astype(jnp.bfloat16)]
    convert_element_type x2 -> x0, local copies, waits for them, and re-layouts: 21.9 us -> none  [shards(): whole_gate, whole_up = (lax.all_to_all(merged_gate.astype(jnp.bfloat16),...]
    unnamed x9 -> x5, local copies, waits for them, and re-layouts: 1.02 us -> 19.1 us
    reduce_sum x4 -> x0, other arithmetic: 14.4 us -> none  [the longest x2 7.2 us: shards(): scale_gate = jnp.sum(jnp.abs(whole_gate), axis=1) / D_MODEL]
    all_to_all x2 -> x0, starting transfers between devices: 11.8 us -> none  [the longest x1 6.35 us: shards(): lax.all_to_all(merged_up.astype(jnp.bfloat16), 'shard', split_axis=0, con...]
  transfers between devices with their start and end apart: 2 -> 0, of which waited for: 1 -> 0; matrix products, arithmetic and copies ran while one was open for 6% -> 0% of each run, Pallas kernels for 0% -> 0%
where the time goes in v1:
time: 591 us
  Pallas kernels  567 us (96%)
  local copies, waits for them, and re-layouts  21.1 us (4%)
    pallas_call x1, Pallas kernels, shards(): pl.pallas_call(functools.partial(exchange, groups, n, each, rows, width),...  567 us
    unnamed x5, local copies, waits for them, and re-layouts  19.1 us

profile of v1, /device:TPU:0, one launch (start us, length us, event | category | flops | bytes accessed | tf_op | source)
XLA Modules:
  0.0 590.6 jit_solution(8807595028251823757)
XLA Ops:
  0.6 1.4 fusion.router
  2.0 567.4 %shard_map.101 = (bf16[4,2048,768]{2,1,0:T(8,128)(2,1)}, bf16[4,2048,768]{2,1,0:T(8,128)(2,1)}, f32[4,1,768]{2,1,0:T(1,128)}, f32[4,1,768]{2,1,0:T(1,128)}, bf16[4,32,2048]{2,1,0:T(8,128)(2,1)}) custom-call(f32[32,256,768]{2,1,0:T(8,128)} %master_gate.1, bf16[32,256,768]{2,1,0:T(8,128)(2,1)} %second_gate.1, f32[32,256,768]{2,1,0:T(8,128)} %master_up.1, ...), custom_call_target="tpu_custom_call" | custom-call | tf_op jit(solution)/shard_map/pallas_call | solution.py:227
  569.4 1.3 copy_bitcast_fusion
  570.7 2.0 copy.11
  572.8 0.0 copy-start
  572.8 11.0 %copy.18 = bf16[4,2048,768]{2,1,0:T(8,128)(2,1)} copy(bf16[4,2048,768]{2,1,0:T(8,128)(2,1)} %get-tuple-element.22) | data formatting | bytes 25165824
  583.8 2.0 copy-done
  585.8 4.8 copy.19
Async XLA Ops:
  572.8 13.0 %copy-start = (bf16[4,2048,768]{2,1,0:T(8,128)(2,1)S(1)}, bf16[4,2048,768]{2,1,0:T(8,128)(2,1)}, u32[]{:S(2)}) copy-start(bf16[4,2048,768]{2,1,0:T(8,128)(2,1)} %get-tuple-element.23) | copy-start | bytes 37748740

commit v2 on v1

--- a/solution.py
+++ b/solution.py
@@ -9,14 +9,15 @@
 
 MESH = pl.DeviceIdType.MESH
 SLOTS = 3
+DELIVER_MIB = 4
 STRIP = 64
 
 
 def exchange(
     groups, n, each, rows, width,
     master_gate, second_gate, master_up, second_up, router,
-    final_gate, final_up, scale_gate, scale_up, routed,
-    land_gate, land_up, out_sem, sent, wide, narrow, in_sem, send_sem, recv_sem, row_send, row_recv, col_send, col_recv,
+    land_gate, land_up, scale_gate, scale_up, routed,
+    sent, wide, narrow, in_sem, send_sem, recv_sem, row_send, row_recv, col_send, col_recv,
 ):
     group, me = lax.axis_index("expert"), lax.axis_index("shard")
     half = n // 2
@@ -28,23 +29,18 @@
     outer = ((chip == 0) | (chip == half - 1)).astype(jnp.int32)
 
     def item(i):
-        cross_start = outer * (each * near)
-        near_start = (1 - outer) * (each * half)
-        is_cross = (i >= cross_start) & (i < cross_start + each * half)
-        is_near = (i >= near_start) & (i < near_start + each * near)
-        is_pair = (i >= each * (n - 2)) & (i < n_remote)
-        q = i - cross_start
-        cross_to = lax.rem(base + half + lax.rem(q + me + n_items, half), n)
-        cross_j = q // half
-        p = i - near_start
-        near_to = base + lax.rem((me - base) // 2 * 2 + 2 + lax.rem(p + n_items * near, near), half)
-        near_j = p // near
+        late = outer * (each * (near + 1))
+        q = i - late
+        own = i >= n_remote
+        early = (i < late) & (outer == 1)
+        span = n - 1
+        k = jnp.where(outer == 1, jnp.where(early, half + lax.rem(i, near + 1), lax.rem(q + span * half, half)), lax.rem(i, span))
+        j = jnp.where(outer == 1, jnp.where(early, i // (near + 1), q // half), i // span)
+        cross_to = lax.rem(base + half + lax.rem(k + me, half), n)
+        near_to = base + lax.rem((me - base) // 2 * 2 + 2 + lax.rem(k + half, near), half)
         pair_to = me + 1 - 2 * lax.rem(me, 2)
-        pair_j = i - each * (n - 2)
-        own_j = i - n_remote
-        target = jnp.where(is_cross, cross_to, jnp.where(is_near, near_to, jnp.where(is_pair, pair_to, me)))
-        j = jnp.where(is_cross, cross_j, jnp.where(is_near, near_j, jnp.where(is_pair, pair_j, own_j)))
-        return target, j
+        target = jnp.where(own, me, jnp.where(k < half, cross_to, jnp.where(k < half + near, near_to, pair_to)))
+        return target, jnp.where(own, i - n_remote, j)
 
     sources = ((master_gate, second_gate), (master_up, second_up))
     lands = (land_gate, land_up)
@@ -107,6 +103,10 @@
             device_id_type=MESH,
         )
 
+    for k in range(n - 1):
+        row_copy(k).start()
+    routed[group, :, my_rows()] = router[...]
+
     def merge(i, put):
         slot = lax.rem(i, SLOTS)
         for t in range(2):
@@ -147,70 +147,90 @@
     lax.fori_loop(0, n_items, produce, 0)
 
     for k in range(n - 1):
-        row_copy(k).start()
-    routed[group, :, my_rows()] = router[...]
-    for k in range(n - 1):
         row_copy(k).wait()
     for k in range(groups - 1):
         col_copy(k).start()
 
     scales = (scale_gate, scale_up)
-    d_model = n * rows
-
-    def put_out(j, t):
-        return pltpu.make_async_copy(lands[t].at[j], (final_gate, final_up)[t].at[j], out_sem.at[j, t])
+
+    def arrive(j, t):
+        def one(k, c):
+            source = lax.rem(me + 1 + k, n)
+            pltpu.make_async_remote_copy(
+                src_ref=sent.at[0, t],
+                dst_ref=lands[t].at[j, pl.ds(pl.multiple_of(source * rows, rows), rows)],
+                send_sem=send_sem.at[0, t],
+                recv_sem=recv_sem.at[j, t, source],
+                device_id=(group, source),
+                device_id_type=MESH,
+            ).wait_recv()
+            return c
+
+        lax.fori_loop(0, n - 1, one, 0)
 
     def finish(j, carry):
         for t in range(2):
-            land = lands[t]
-
-            def arrive(k, c, t=t):
-                source = lax.rem(me + 1 + k, n)
-                pltpu.make_async_remote_copy(
-                    src_ref=sent.at[0, t],
-                    dst_ref=lands[t].at[j, pl.ds(pl.multiple_of(source * rows, rows), rows)],
-                    send_sem=send_sem.at[0, t],
-                    recv_sem=recv_sem.at[j, t, source],
-                    device_id=(group, source),
-                    device_id_type=MESH,
-                ).wait_recv()
-                return c
-
-            lax.fori_loop(0, n - 1, arrive, 0)
-
-            def add(s, total, land=land):
-                at = pl.ds(pl.multiple_of(s * STRIP, STRIP), STRIP)
-                block = jnp.abs(land[j, at, :].astype(jnp.float32))
-                return total + jnp.sum(block.reshape(STRIP // 8, 8, width), axis=0)
-
-            total = lax.fori_loop(0, d_model // STRIP, add, jnp.zeros((8, width), jnp.float32))
-            scale = jnp.sum(total, axis=0, keepdims=True) / d_model
-            scales[t][j] = scale
-            factor = jnp.broadcast_to(1.0 / scale, (STRIP, width))
-
-            def divide(s, c, land=land, factor=factor):
-                at = pl.ds(pl.multiple_of(s * STRIP, STRIP), STRIP)
-                land[j, at, :] = (land[j, at, :].astype(jnp.float32) * factor).astype(jnp.bfloat16)
-                return c
-
-            lax.fori_loop(0, d_model // STRIP, divide, 0)
-            put_out(j, t).start()
+            arrive(j, t)
+            scales[t][j] = normalise(lands[t].at[j], lands[t].at[j])
         return carry
 
     lax.fori_loop(0, each, finish, 0)
 
     for k in range(groups - 1):
         col_copy(k).wait()
-
     def drain(i, carry):
         for copy in sends(i):
             copy.wait_send()
         return carry
 
     lax.fori_loop(0, n_remote, drain, 0)
-    for j in range(each):
-        for t in range(2):
-            put_out(j, t).wait()
+
+
+def normalise(source, target):
+    depth, width = source.shape
+
+    def add(s, total):
+        block = jnp.abs(source[pl.ds(pl.multiple_of(s * STRIP, STRIP), STRIP), :].astype(jnp.float32))
+        return total + jnp.sum(block.reshape(STRIP // 8, 8, width), axis=0)
+
+    total = lax.fori_loop(0, depth // STRIP, add, jnp.zeros((8, width), jnp.float32))
+    scale = jnp.sum(total, axis=0, keepdims=True) / depth
+    factor = jnp.broadcast_to(1.0 / scale, (STRIP, width))
+
+    def divide(s, c):
+        at = pl.ds(pl.multiple_of(s * STRIP, STRIP), STRIP)
+        target[at, :] = (source[at, :].astype(jnp.float32) * factor).astype(jnp.bfloat16)
+        return c
+
+    lax.fori_loop(0, depth // STRIP, divide, 0)
+    return scale
+
+
+def deliver(
+    each, land_gate, land_up, part_gate, part_up, routed,
+    final_gate, final_up, scale_gate, scale_up, serve_router,
+    turned, sem, turned_sem,
+):
+    tensors = ((land_gate, part_gate, final_gate, scale_gate), (land_up, part_up, final_up, scale_up))
+    copies = [
+        pltpu.make_async_copy(tensors[t][0].at[j], tensors[t][2].at[j], sem.at[j, t])
+        for j in range(each)
+        for t in range(2)
+    ]
+    for copy in copies:
+        copy.start()
+    for t, (land, part, final, scale) in enumerate(tensors):
+        for j in range(each):
+            scale[j:j + 1, :] = part[j]
+    side = routed.shape[0]
+    for c in range(routed.shape[1] // side):
+        at = slice(c * side, (c + 1) * side)
+        turned[at, :] = routed[:, at].astype(jnp.float32).T.astype(jnp.bfloat16)
+    copy = pltpu.make_async_copy(turned, serve_router, turned_sem.at[0])
+    copy.start()
+    copies.append(copy)
+    for copy in copies:
+        copy.wait()
 
 
 def shards(groups, n, master_gate, second_gate, master_up, second_up, router_weight, router_gain):
@@ -220,19 +240,16 @@
     router = (router_weight * router_gain[:, None]).astype(jnp.bfloat16).T
     land = pltpu.VMEM((each, n * rows, width), jnp.bfloat16)
     final = jax.ShapeDtypeStruct((each, n * rows, width), jnp.bfloat16)
-    scale = jax.ShapeDtypeStruct((each, 1, width), jnp.float32)
+    scale = pltpu.VMEM((each, 1, width), jnp.float32)
     vmem = pl.BlockSpec(memory_space=pltpu.VMEM)
     hbm = pl.BlockSpec(memory_space=pltpu.HBM)
     remote = each * (n - 1)
-    final_gate, final_up, scale_gate, scale_up, routed = pl.pallas_call(
+    land_gate, land_up, part_gate, part_up, routed = pl.pallas_call(
         functools.partial(exchange, groups, n, each, rows, width),
-        out_shape=(final, final, scale, scale, jax.ShapeDtypeStruct((groups, columns, n * rows), jnp.bfloat16)),
+        out_shape=(land, land, scale, scale, pltpu.VMEM((groups, columns, n * rows), jnp.bfloat16)),
         in_specs=[hbm] * 4 + [vmem],
-        out_specs=(hbm, hbm, vmem, vmem, vmem),
+        out_specs=(vmem,) * 5,
         scratch_shapes=[
-            land,
-            land,
-            pltpu.SemaphoreType.DMA((each, 2)),
             pltpu.VMEM((remote, 2, rows, width), jnp.bfloat16),
             pltpu.VMEM((SLOTS, 2, rows, width), jnp.float32),
             pltpu.VMEM((SLOTS, 2, rows, width), jnp.bfloat16),
@@ -245,14 +262,23 @@
             pltpu.SemaphoreType.DMA((groups - 1,)),
         ],
         compiler_params=pltpu.CompilerParams(
-            collective_id=0, has_side_effects=True, vmem_limit_bytes=60 * 1024 * 1024
+            collective_id=0, has_side_effects=True, vmem_limit_bytes=32 * 1024 * 1024
         ),
     )(master_gate, second_gate, master_up, second_up, router)
-    serve_router = routed.reshape(groups * columns, n * rows).T
-    return (
-        final_gate, final_up,
-        scale_gate.reshape(each, width), scale_up.reshape(each, width), serve_router,
-    )
+    experts_all, model = groups * columns, n * rows
+    total = jax.ShapeDtypeStruct((each, width), jnp.float32)
+    return pl.pallas_call(
+        functools.partial(deliver, each),
+        out_shape=(final, final, total, total, jax.ShapeDtypeStruct((model, experts_all), jnp.bfloat16)),
+        in_specs=[pl.BlockSpec(memory_space=pl.ANY)] * 2 + [vmem] * 3,
+        out_specs=(hbm, hbm, vmem, vmem, hbm),
+        scratch_shapes=[
+            pltpu.VMEM((model, experts_all), jnp.bfloat16),
+            pltpu.SemaphoreType.DMA((each, 2)),
+            pltpu.SemaphoreType.DMA((1,)),
+        ],
+        compiler_params=pltpu.CompilerParams(vmem_limit_bytes=DELIVER_MIB * 1024 * 1024),
+    )(land_gate, land_up, part_gate, part_up, routed.reshape(experts_all, model))
 
 
 def solution(mesh):

time: 591 us -> 563 us (0.953)
  local copies, waits for them, and re-layouts: 21.1 us -> 0 us
  Pallas kernels: 567 us -> 561 us
    unnamed x5 -> x0, local copies, waits for them, and re-layouts: 19.1 us -> none
    pallas_call x1, Pallas kernels: 567 us -> 552 us  [shards(): pl.pallas_call(functools.partial(exchange, groups, n, each, rows, width),...]
    pallas_call x0 -> x1, Pallas kernels: none -> 9.24 us  [shards(): pl.pallas_call(functools.partial(deliver, each), out_shape=(final, final,...]
where the time goes in v2:
time: 563 us
  Pallas kernels  561 us (100%)
    pallas_call x1, Pallas kernels, shards(): pl.pallas_call(functools.partial(exchange, groups, n, each, rows, width),...  552 us

profile of v2, /device:TPU:0, one launch (start us, length us, event | category | flops | bytes accessed | tf_op | source)
XLA Modules:
  0.0 563.2 jit_solution(4657986658160815533)
XLA Ops:
  0.6 1.4 fusion.router
  2.0 551.9 %shard_map.101 = (bf16[4,2048,768]{2,1,0:T(8,128)(2,1)S(1)}, bf16[4,2048,768]{2,1,0:T(8,128)(2,1)S(1)}, f32[4,1,768]{2,1,0:T(1,128)S(1)}, f32[4,1,768]{2,1,0:T(1,128)S(1)}, bf16[4,32,2048]{2,1,0:T(8,128)(2,1)S(1)}) custom-call(f32[32,256,768]{2,1,0:T(8,128)} %master_gate.1, bf16[32,256,768]{2,1,0:T(8,128)(2,1)} %second_gate.1, f32[32,256,768]{2,1,0:T(8,128)} %master_up.1, ...), custom_call_target="tpu_custom_call" | custom-call | tf_op jit(solution)/shard_map/pallas_call | solution.py:247
  553.9 9.2 %shard_map.102 = (bf16[4,2048,768]{2,1,0:T(8,128)(2,1)}, bf16[4,2048,768]{2,1,0:T(8,128)(2,1)}, f32[4,768]{1,0:T(4,128)}, f32[4,768]{1,0:T(4,128)}, bf16[2048,128]{1,0:T(8,128)(2,1)}) custom-call(bf16[4,2048,768]{2,1,0:T(8,128)(2,1)S(1)} %get-tuple-element.10.land_gate, bf16[4,2048,768]{2,1,0:T(8,128)(2,1)S(1)} %get-tuple-element.11.land_up, ...), custom_call_target="tpu_custom_call" | custom-call | tf_op jit(solution)/shard_map/pallas_call | solution.py:270
